TPU v7x, 32 devices: a whole 2x2x4 slice. The times are simulated.
32 devices in a mesh: row: 8 (over y, x, core), col: 4 (over z).
Axes of the slice: x: 2, y: 2, z: 4, core: 2. Of those that a mesh axis runs over, the one named last changes fastest.
Arguments:
- points: float32 [64, 8192], P(None, ('row', 'col')), may hold values from -6 to 6
- labels: int32 [64], P(('row', 'col')), may hold values from 0 to 1
- solution: float32 [8192], P(('row', 'col')), may hold values from -6 to 6
- residual: float32 [8192], P(('row', 'col')), may hold values from -6 to 6
- direction: float32 [8192], P(('row', 'col')), may hold values from -6 to 6
- len_low: float32 [64], replicated, may hold values from 0.75 to 40
- len_high: float32 [64], replicated, may hold values from 0.9 to 40
- variances: float32 [2], replicated, may hold values from 0.5 to 2
- nugget: float32 [2], replicated, may hold values from 0.3 to 1.5
- coupling: float32 [1], replicated, may hold values from 0.6 to 1.6
Outputs:
- solution_next: float32 [8192], P(('row', 'col'))
- residual_next: float32 [8192], P(('row', 'col'))
- direction_next: float32 [8192], P(('row', 'col'))
All inputs are finite; a program needn't handle non-finite values.
Results may differ from a plain program's by a relative error of at most 0.00027.
Values sent between devices are 32-bit elements; how exact they have to be, the bound alone decides.
A program may use at most 64 MiB of HBM per device.

v0:
```python
import jax
import jax.numpy as jnp
from jax import lax
from jax.sharding import PartitionSpec as P


def scale_factors(fidelity, coupling):
    return 1.0 + (coupling[0] - 1.0) * fidelity


def kernel_terms(
    totals,
    rows_low,
    rows_high,
    norms_low,
    norms_high,
    col_low,
    col_high,
    col_label,
    col_dir,
    coupling,
):
    col_width = col_low.shape[1]
    block_width = col_width
    while block_width > 1024 and block_width % 2 == 0:
        block_width = block_width // 2
    dims = (((0,), (0,)), ((), ()))

    def one_block(block_index, accumulated):
        offset = block_index * block_width
        part_low = lax.dynamic_slice_in_dim(col_low, offset, block_width, 1)
        part_high = lax.dynamic_slice_in_dim(col_high, offset, block_width, 1)
        part_label = lax.dynamic_slice_in_dim(col_label, offset, block_width, 1)[0]
        part_dir = lax.dynamic_slice_in_dim(col_dir, offset, block_width, 1)[0]
        part_nlow = jnp.sum(part_low * part_low, 0)
        part_nhigh = jnp.sum(part_high * part_high, 0)
        dist_low = (
            norms_low[:, None]
            + part_nlow[None, :]
            - 2.0 * lax.dot_general(rows_low, part_low, dims, precision=lax.Precision.HIGHEST)
        )
        dist_high = (
            norms_high[:, None]
            + part_nhigh[None, :]
            - 2.0 * lax.dot_general(rows_high, part_high, dims, precision=lax.Precision.HIGHEST)
        )
        weights_low = scale_factors(part_label, coupling) * part_dir
        weights_high = part_label * part_dir
        next_low = accumulated[0] + jnp.dot(
            jnp.exp(-0.5 * dist_low), weights_low, precision=lax.Precision.HIGHEST
        )
        next_high = accumulated[1] + jnp.dot(
            jnp.exp(-0.5 * dist_high), weights_high, precision=lax.Precision.HIGHEST
        )
        return (next_low, next_high)

    return lax.fori_loop(0, col_width // block_width, one_block, totals)


def body(
    points, labels, solution, residual, direction, len_low, len_high, variances, nugget, coupling
):
    own_width = points.shape[1]
    own_label = jnp.repeat(labels, 128).astype(jnp.float32)
    label_row = own_label[None, :]
    dir_row = direction[None, :]
    own_low = points / len_low[:, None]
    own_high = points / len_high[:, None]
    rows_low, rows_high, rows_label = (
        lax.all_gather(own_low, "col", axis=1, tiled=True),
        lax.all_gather(own_high, "col", axis=1, tiled=True),
        lax.all_gather(label_row, "col", axis=1, tiled=True),
    )
    norms_low = jnp.sum(rows_low * rows_low, 0)
    norms_high = jnp.sum(rows_high * rows_high, 0)
    zeros_rows = jnp.zeros((rows_low.shape[1],), jnp.float32)
    sum_low, sum_high = kernel_terms(
        (zeros_rows, zeros_rows),
        rows_low,
        rows_high,
        norms_low,
        norms_high,
        lax.all_gather(own_low, "row", axis=1, tiled=True),
        lax.all_gather(own_high, "row", axis=1, tiled=True),
        lax.all_gather(label_row, "row", axis=1, tiled=True),
        lax.all_gather(dir_row, "row", axis=1, tiled=True),
        coupling,
    )
    rows_fidelity = rows_label[0]
    row_terms = (
        variances[0] * scale_factors(rows_fidelity, coupling) * sum_low
        + variances[1] * rows_fidelity * sum_high
    )
    summed = lax.psum(row_terms, "col")
    own_terms = lax.dynamic_slice_in_dim(summed, lax.axis_index("col") * own_width, own_width, 0)
    nugget_points = nugget[0] + (nugget[1] - nugget[0]) * own_label
    kernel_image = own_terms + nugget_points * direction
    old_norm, curvature, cross_term, image_norm = lax.psum(
        (
            jnp.sum(residual * residual),
            jnp.sum(direction * kernel_image),
            jnp.sum(residual * kernel_image),
            jnp.sum(kernel_image * kernel_image),
        ),
        ("row", "col"),
    )
    step_size = old_norm / curvature
    solution_next = solution + step_size * direction
    residual_next = residual - step_size * kernel_image
    new_norm = old_norm - 2.0 * step_size * cross_term + step_size * step_size * image_norm
    direction_next = residual_next + new_norm / old_norm * direction
    return (solution_next, residual_next, direction_next)


def solution(mesh):
    placed = (
        P(None, ("row", "col")),
        P(("row", "col")),
        P(("row", "col")),
        P(("row", "col")),
        P(("row", "col")),
        P(),
        P(),
        P(),
        P(),
        P(),
    )
    return jax.shard_map(
        body,
        mesh=mesh,
        in_specs=placed,
        out_specs=(P(("row", "col")), P(("row", "col")), P(("row", "col"))),
        check_vma=False,
    )
```

profile of v0, /device:TPU:0, one launch (start us, length us, event | category | flops | bytes accessed | tf_op | source)
XLA Modules:
  0.0 171.4 jit_solution(8443081240500379982)
XLA Ops:
  0.6 0.9 broadcast_divide_fusion
  1.6 15.7 %all_gather.26 = f32[64,1024]{1,0:T(8,128)S(1)} all-gather(f32[64,256]{1,0:T(8,128)S(1)} %get-tuple-element.362), channel_id=1, replica_groups=mesh['row'=8,'col'=4] {'col'}, dimensions={1}, use_global_device_ids=true | all-gather | bytes 327680 | tf_op jit(solution)/shard_map/all_gather | solution.py:71
  17.3 14.6 %all_gather.22 = f32[64,1024]{1,0:T(8,128)S(1)} all-gather(f32[64,256]{1,0:T(8,128)S(1)} %get-tuple-element.363), channel_id=1, replica_groups=mesh['row'=8,'col'=4] {'col'}, dimensions={1}, use_global_device_ids=true | all-gather | bytes 327680 | tf_op jit(solution)/shard_map/all_gather | solution.py:70
  31.9 9.9 %all_gather.23 = f32[64,2048]{1,0:T(8,128)S(1)} all-gather(f32[64,256]{1,0:T(8,128)S(1)} %get-tuple-element.363), channel_id=1, replica_groups=mesh['row'=8,'col'=4] {'row'}, dimensions={1}, use_global_device_ids=true | all-gather | bytes 589824 | tf_op jit(solution)/shard_map/all_gather | solution.py:83
  41.8 9.8 %all_gather.27 = f32[64,2048]{1,0:T(8,128)S(1)} all-gather(f32[64,256]{1,0:T(8,128)S(1)} %get-tuple-element.362), channel_id=1, replica_groups=mesh['row'=8,'col'=4] {'row'}, dimensions={1}, use_global_device_ids=true | all-gather | bytes 589824 | tf_op jit(solution)/shard_map/all_gather | solution.py:84
  51.6 0.7 convert_element_type.16
  52.3 7.9 %all_gather.24 = f32[1,2048]{1,0:T(1,128)S(1)} all-gather(f32[1,256]{1,0:T(1,128)S(1)} %bitcast.73), channel_id=1, replica_groups=mesh['row'=8,'col'=4] {'row'}, dimensions={1}, use_global_device_ids=true | all-gather | bytes 9216 | tf_op jit(solution)/shard_map/all_gather | solution.py:85
  60.9 8.9 %all-gather.1 = f32[8,1,256]{2,1,0:T(1,128)S(1)} all-gather(f32[1,1,256]{2,1,0:T(1,128)} %bitcast.72), channel_id=2, replica_groups=mesh['row'=8,'col'=4] {'row'}, dimensions={0}, use_global_device_ids=true | all-gather | bytes 9216 | tf_op jit(solution)/shard_map/all_gather | solution.py:86
  69.8 32.6 %while.18 = (s32[]{:T(128)}, f32[1024]{0:T(1024)S(1)}, f32[1024]{0:T(1024)S(1)}, f32[1024]{0:T(1024)S(1)}, f32[64,2048]{1,0:T(8,128)S(1)}, /*index=5*/f32[64,102...) while((s32[]{:T(128)}, f32[1024]{0:T(1024)S(1)}, ...), condition=%wide.region_7.0_spmd.clone, body=%wide.region_4.7_spmd.clone.sunk | while | flops 1644435456 | bytes 18448608 | solution.py:57
  70.1 3.5 %fusion.63 = f32[1024,1024]{0,1:T(8,128)S(1)} fusion(f32[64,1024]{1,0:T(8,128)S(1)} %get-tuple-element.499, f32[64,2048]{1,0:T(8,128)S(1)} %get-tuple-element.498, s32[]{:T(128)S(6)} %select_n.18), kind=kOutput, calls=%fused_computation.22.clone.1 | convolution fusion | flops 805306368 | bytes 4718596 | tf_op jit(solution)/shard_map/while/body/eval_jaxpr/dot_general | solution.py:45
  73.7 4.5 %fusion.64 = f32[1,1024]{1,0:T(1,128)S(1)} fusion(f32[1024,1]{0,1:T(1,128)S(1)} %bitcast.68, f32[1024,1024]{0,1:T(8,128)S(1)} %fusion.63, f32[1024]{0:T(1024)S(1)} %get-tuple-element.455, f32[1024]{0:T(1024)S(1)} %get-tuple-element.497), kind=kOutput, calls=%fused_computation.3.clone.1 | convolution fusion | flops 16777216 | bytes 4210688 | tf_op jit(solution)/shard_map/while/body/eval_jaxpr/dot_general | solution.py:52
  78.2 3.5 %fusion.61 = f32[1024,1024]{0,1:T(8,128)S(1)} fusion(f32[64,1024]{1,0:T(8,128)S(1)} %get-tuple-element.493, f32[64,2048]{1,0:T(8,128)S(1)} %get-tuple-element.492, s32[]{:T(128)S(6)} %select_n.18), kind=kOutput, calls=%fused_computation.24.clone.1 | convolution fusion | flops 805306368 | bytes 4718596 | tf_op jit(solution)/shard_map/while/body/eval_jaxpr/dot_general | solution.py:40
  81.7 4.5 %fusion.62 = f32[1,1024]{1,0:T(1,128)S(1)} fusion(f32[1024,1]{0,1:T(1,128)S(1)} %bitcast.67, f32[1024,1024]{0,1:T(8,128)S(1)} %fusion.61, f32[1024]{0:T(1024)S(1)} %get-tuple-element.453, f32[1024]{0:T(1024)S(1)} %get-tuple-element.491), kind=kOutput, calls=%fused_computation.7.clone.1 | convolution fusion | flops 16777216 | bytes 4210688 | tf_op jit(solution)/shard_map/while/body/eval_jaxpr/dot_general | solution.py:49
  86.3 3.5 %fusion.63 = f32[1024,1024]{0,1:T(8,128)S(1)} fusion(f32[64,1024]{1,0:T(8,128)S(1)} %get-tuple-element.499, f32[64,2048]{1,0:T(8,128)S(1)} %get-tuple-element.498, s32[]{:T(128)S(6)} %select_n.18), kind=kOutput, calls=%fused_computation.22.clone.1 | convolution fusion | flops 805306368 | bytes 4718596 | tf_op jit(solution)/shard_map/while/body/eval_jaxpr/dot_general | solution.py:45
  89.9 4.5 %fusion.64 = f32[1,1024]{1,0:T(1,128)S(1)} fusion(f32[1024,1]{0,1:T(1,128)S(1)} %bitcast.68, f32[1024,1024]{0,1:T(8,128)S(1)} %fusion.63, f32[1024]{0:T(1024)S(1)} %get-tuple-element.455, f32[1024]{0:T(1024)S(1)} %get-tuple-element.497), kind=kOutput, calls=%fused_computation.3.clone.1 | convolution fusion | flops 16777216 | bytes 4210688 | tf_op jit(solution)/shard_map/while/body/eval_jaxpr/dot_general | solution.py:52
  94.4 3.5 %fusion.61 = f32[1024,1024]{0,1:T(8,128)S(1)} fusion(f32[64,1024]{1,0:T(8,128)S(1)} %get-tuple-element.493, f32[64,2048]{1,0:T(8,128)S(1)} %get-tuple-element.492, s32[]{:T(128)S(6)} %select_n.18), kind=kOutput, calls=%fused_computation.24.clone.1 | convolution fusion | flops 805306368 | bytes 4718596 | tf_op jit(solution)/shard_map/while/body/eval_jaxpr/dot_general | solution.py:40
  97.9 4.5 %fusion.62 = f32[1,1024]{1,0:T(1,128)S(1)} fusion(f32[1024,1]{0,1:T(1,128)S(1)} %bitcast.67, f32[1024,1024]{0,1:T(8,128)S(1)} %fusion.61, f32[1024]{0:T(1024)S(1)} %get-tuple-element.453, f32[1024]{0:T(1024)S(1)} %get-tuple-element.491), kind=kOutput, calls=%fused_computation.7.clone.1 | convolution fusion | flops 16777216 | bytes 4210688 | tf_op jit(solution)/shard_map/while/body/eval_jaxpr/dot_general | solution.py:49
  102.4 10.9 %all_gather.21 = f32[1,1024]{1,0:T(1,128)S(1)} all-gather(f32[1,256]{1,0:T(1,128)S(1)} %bitcast.74), channel_id=1, replica_groups=mesh['row'=8,'col'=4] {'col'}, dimensions={1}, use_global_device_ids=true | all-gather | bytes 5120 | tf_op jit(solution)/shard_map/all_gather | solution.py:72
  113.3 0.6 fusion.33
  113.9 1.3 add_multiply_fusion.1
  115.2 8.4 %psum.36 = f32[1024]{0:T(1024)S(1)} all-reduce(f32[1024]{0:T(1024)S(1)} %multiply_add_fusion), channel_id=1, replica_groups=mesh['row'=8,'col'=4] {'col'}, use_global_device_ids=true, to_apply=%region_8.0 | all-reduce | flops 1024 | bytes 8192 | tf_op jit(solution)/shard_map/psum | solution.py:94
  125.5 0.7 multiply_add_fusion.3
  126.1 0.8 multiply_reduce_fusion.4
  126.9 40.0 %all-reduce = (f32[]{:T(128)}, f32[]{:T(128)}, f32[]{:T(128)}, f32[]{:T(128)}) all-reduce(f32[]{:T(128)} %get-tuple-element.323, f32[]{:T(128)} %get-tuple-element.324, f32[]{:T(128)} %get-tuple-element.322, f32[]{:T(128)} %get-tuple-element.321), channel_id=1, replica_groups=mesh['row'=8,'col'=4] {'row','col'}, use_global_device_ids=true, to_apply=%region_1.0 | all-reduce | flops 4 | bytes 32 | tf_op jit(solution)/shard_map/psum | solution.py:98
  (30 shorter events, 1.5 us)
Async XLA Ops:
  69.8 43.5 %copy-start.2 = (f32[2]{0:T(128)S(1)}, f32[2]{0:T(128)}, u32[]{:S(2)}) copy-start(f32[2]{0:T(128)} %param.19) | copy-start | bytes 28
  69.8 53.8 %copy-start.3 = (f32[2]{0:T(128)S(1)}, f32[2]{0:T(128)}, u32[]{:S(2)}) copy-start(f32[2]{0:T(128)} %param.20) | copy-start | bytes 28
  69.8 55.6 %copy-start.5 = (s32[2]{0:T(128)S(1)}, s32[2]{0:T(128)}, u32[]{:S(2)}) copy-start(s32[2]{0:T(128)} %param.13) | copy-start | bytes 28
  69.8 56.3 %copy-start = (f32[256]{0:T(256)S(1)}, f32[256]{0:T(256)}, u32[]{:S(2)}) copy-start(f32[256]{0:T(256)} %param.16) | copy-start | bytes 3076
  69.8 56.3 %copy-start.1 = (f32[256]{0:T(256)S(1)}, f32[256]{0:T(256)}, u32[]{:S(2)}) copy-start(f32[256]{0:T(256)} %param.15) | copy-start | bytes 3076
  69.8 101.0 %copy-start.4 = (f32[256]{0:T(256)S(1)}, f32[256]{0:T(256)}, u32[]{:S(2)}) copy-start(f32[256]{0:T(256)} %param.14) | copy-start | bytes 3076
where the time goes:
time: 172 us; the launch traced here: 171 us
  blocking collectives  126 us (73%)
  matrix products  32.1 us (19%)
  between operations  6.56 us (4%)
  other arithmetic  5.15 us (3%)
    psum x1, blocking collectives, body(): lax.psum((jnp.sum(residual * residual), jnp.sum(direction * kernel_image)...  40 us
    all_gather x1, blocking collectives, body(): lax.all_gather(own_high, 'col', axis=1, tiled=True)  15.7 us
    all_gather x1, blocking collectives, body(): lax.all_gather(own_low, 'col', axis=1, tiled=True)  14.6 us
    all_gather x1, blocking collectives, body(): lax.all_gather(label_row, 'col', axis=1, tiled=True)  10.9 us
    all_gather x1, blocking collectives, body(): lax.all_gather(own_low, 'row', axis=1, tiled=True)  9.86 us
    all_gather x1, blocking collectives, body(): lax.all_gather(own_high, 'row', axis=1, tiled=True)  9.81 us
    dot_general x2, matrix products, one_block(): jnp.dot(jnp.exp(-0.5 * dist_low), weights_low, precision=lax.Precision.HI...  8.99 us
    dot_general x2, matrix products, one_block(): jnp.dot(jnp.exp(-0.5 * dist_high), weights_high, precision=lax.Precision....  8.97 us

commit v1 on v0

v1 whole, which is shorter than its diff:
```python
import functools
import math

import jax
import jax.numpy as jnp
from jax import lax
from jax.experimental import pallas as pl
from jax.experimental.pallas import tpu as pltpu
from jax.sharding import PartitionSpec as P

MESH = pl.DeviceIdType.MESH
LANES = 128
ROOT_LOG2E = math.sqrt(math.log2(math.e))


def peer_of(index, offset, count):
    if count & (count - 1):
        return lax.rem(index + offset, count)
    peer, bit = index, 1
    while bit < count:
        if offset & bit:
            peer = peer + bit * (1 - 2 * ((index // bit) % 2))
        bit *= 2
    return peer


def as_column(row):
    n = row.shape[1]
    diagonal = lax.broadcasted_iota(jnp.int32, (n, n), 0) == lax.broadcasted_iota(
        jnp.int32, (n, n), 1
    )
    return jnp.sum(jnp.where(diagonal, jnp.broadcast_to(row, (n, n)), 0.0), axis=1, keepdims=True)


def two_terms(value):
    hi = value.astype(jnp.bfloat16)
    lo = (value - hi.astype(jnp.float32)).astype(jnp.bfloat16)
    whole = hi.astype(jnp.float32) + lo.astype(jnp.float32)
    return hi, lo, whole


def kernel(
    row_count,
    col_count,
    points_ref,
    labels_ref,
    solution_ref,
    residual_ref,
    direction_ref,
    len_low_ref,
    len_high_ref,
    variances_ref,
    nugget_ref,
    coupling_ref,
    solution_out,
    residual_out,
    direction_out,
    col_buf,
    row_buf,
    lhs,
    rhs,
    col_bias,
    col_weight,
    part_buf,
    sums_buf,
    row_send,
    row_recv,
    col_send,
    col_recv,
    part_send,
    part_recv,
    sums_send,
    sums_recv,
):
    me_row, me_col = lax.axis_index("row"), lax.axis_index("col")
    features, width = points_ref.shape
    row_peers = [(d, (peer_of(me_row, d, row_count), me_col)) for d in range(1, row_count)]
    col_peers = [(d, (me_row, peer_of(me_col, d, col_count))) for d in range(1, col_count)]

    barrier = pltpu.get_barrier_semaphore()
    for _, peer in row_peers + col_peers:
        pl.semaphore_signal(barrier, inc=1, device_id=peer, device_id_type=MESH)

    own = col_buf.at[0]
    lane = lax.broadcasted_iota(jnp.int32, (1, width), 1)
    fidelity = jnp.zeros((1, width), jnp.float32)
    for block in range(labels_ref.shape[0]):
        fidelity = jnp.where(
            lane // LANES == block, labels_ref[block].astype(jnp.float32), fidelity
        )
    own[:features, :] = points_ref[...]
    own[features:, :] = jnp.concatenate(
        [fidelity, direction_ref[...], residual_ref[...], jnp.zeros((5, width), jnp.float32)], 0
    )
    row_buf[0] = own[...]

    pl.semaphore_wait(barrier, len(row_peers) + len(col_peers))

    sends = []
    for d, peer in col_peers:
        sends.append(
            pltpu.make_async_remote_copy(
                src_ref=own,
                dst_ref=row_buf.at[d],
                send_sem=col_send.at[d],
                recv_sem=col_recv.at[d],
                device_id=peer,
                device_id_type=MESH,
            )
        )
        sends[-1].start()
    col_copies = dict(zip([d for d, _ in col_peers], sends))
    row_copies = {}
    for d, peer in row_peers:
        copy = pltpu.make_async_remote_copy(
            src_ref=own,
            dst_ref=col_buf.at[d],
            send_sem=row_send.at[d],
            recv_sem=row_recv.at[d],
            device_id=peer,
            device_id_type=MESH,
        )
        copy.start()
        row_copies[d] = copy

    inverse = [ROOT_LOG2E / len_low_ref[...], ROOT_LOG2E / len_high_ref[...]]
    lane_scale = [jnp.concatenate([value, value], 1) for value in inverse]
    column_scale = [as_column(value) for value in inverse]
    coupling = coupling_ref[0]

    def prepare_rows(d):
        raw = row_buf[d, :features, :]
        for which in range(2):
            hi, lo, whole = two_terms(raw * column_scale[which])
            rhs[which] = jnp.concatenate([hi, lo, hi, lo], 0)
            yield -0.5 * jnp.sum(whole * whole, 0, keepdims=True)

    def prepare_columns(d):
        raw = col_buf[d, :features, :]
        turned = jnp.concatenate([raw, raw], 0).T
        extra = jnp.concatenate(
            [col_buf[d, features:, :], jnp.zeros((LANES - 8, width), jnp.float32)], 0
        ).T
        label, step_dir = extra[:, 0:1], extra[:, 1:2]
        weights = [(1.0 + (coupling - 1.0) * label) * step_dir, label * step_dir]
        for which in range(2):
            hi, lo, whole = two_terms(turned * lane_scale[which])
            lhs[which, d] = jnp.concatenate([hi, lo], 1)
            bias = -0.25 * jnp.sum(whole * whole, 1, keepdims=True)
            col_bias[which, d] = jnp.broadcast_to(bias, (width, LANES))
            col_weight[which, d] = jnp.broadcast_to(weights[which], (width, LANES))

    def accumulate(d, row_bias, totals):
        result = []
        for which in range(2):
            power = jnp.dot(lhs[which, d], rhs[which], preferred_element_type=jnp.float32)
            bias, weight = col_bias[which, d], col_weight[which, d]
            halves = []
            for at in range(0, width, LANES):
                value = (
                    jnp.exp2(power[:, at : at + LANES] + bias + row_bias[which][:, at : at + LANES])
                    * weight
                )
                halves.append(jnp.sum(value.reshape(width // 8, 8, LANES), 0))
            result.append(totals[which] + jnp.concatenate(halves, 1))
        return tuple(result)

    zeros = jnp.zeros((8, width), jnp.float32)

    def finish(d, totals):
        label = row_buf[d, features : features + 1, :]
        low = jnp.sum(totals[0], 0, keepdims=True)
        high = jnp.sum(totals[1], 0, keepdims=True)
        part_buf[0, d : d + 1, :] = (
            variances_ref[0] * (1.0 + (coupling - 1.0) * label) * low
            + variances_ref[1] * label * high
        )

    row_bias = list(prepare_rows(0))
    totals = (zeros, zeros)
    prepare_columns(0)
    totals = accumulate(0, row_bias, totals)
    for d in range(1, row_count):
        row_copies[d].wait_recv()
        prepare_columns(d)
        totals = accumulate(d, row_bias, totals)
    finish(0, totals)
    for c in range(1, col_count):
        col_copies[c].wait_recv()
        row_bias = list(prepare_rows(c))
        totals = lax.fori_loop(
            0, row_count, lambda d, t: accumulate(d, row_bias, t), (zeros, zeros)
        )
        finish(c, totals)

    part_copies = []
    for d, peer in col_peers:
        copy = pltpu.make_async_remote_copy(
            src_ref=part_buf.at[0],
            dst_ref=part_buf.at[d],
            send_sem=part_send.at[d],
            recv_sem=part_recv.at[d],
            device_id=peer,
            device_id_type=MESH,
        )
        copy.start()
        part_copies.append(copy)

    first, second = nugget_ref[0], nugget_ref[1]
    images, labels_of, dirs, resids = [], [], [], []
    for d in range(col_count):
        labels_of.append(row_buf[d, features : features + 1, :])
        dirs.append(row_buf[d, features + 1 : features + 2, :])
        resids.append(row_buf[d, features + 2 : features + 3, :])
        images.append(
            part_buf[0, d : d + 1, :] + (first + (second - first) * labels_of[d]) * dirs[d]
        )
    for d, copy in enumerate(part_copies, 1):
        copy.wait_recv()
        for e in range(col_count):
            if col_count & (col_count - 1):
                place = (e - d) % col_count
                images[e] = images[e] + part_buf[d, place : place + 1, :]
            else:
                images[e] = images[e] + part_buf[d, (d ^ e) : (d ^ e) + 1, :]

    def line_sum(left, right):
        total = sum(a * b for a, b in zip(left, right))
        return sum(total[:, at : at + LANES] for at in range(0, width, LANES))

    sums_buf[0] = jnp.concatenate(
        [
            line_sum(resids, resids),
            line_sum(dirs, images),
            line_sum(resids, images),
            line_sum(images, images),
            jnp.zeros((4, LANES), jnp.float32),
        ],
        0,
    )
    sums_copies = []
    for d, peer in row_peers:
        copy = pltpu.make_async_remote_copy(
            src_ref=sums_buf.at[0],
            dst_ref=sums_buf.at[d],
            send_sem=sums_send.at[d],
            recv_sem=sums_recv.at[d],
            device_id=peer,
            device_id_type=MESH,
        )
        copy.start()
        sums_copies.append(copy)
    sums = sums_buf[0]
    for d, copy in enumerate(sums_copies, 1):
        copy.wait_recv()
        sums = sums + sums_buf[d]
    sums = jnp.sum(sums, 1, keepdims=True)
    old_norm, curvature = sums[0:1], sums[1:2]
    cross_term, image_norm = sums[2:3], sums[3:4]
    step_size = old_norm / curvature
    new_norm = old_norm - 2.0 * step_size * cross_term + step_size * step_size * image_norm
    residual_next = resids[0] - step_size * images[0]
    solution_out[...] = solution_ref[...] + step_size * dirs[0]
    residual_out[...] = residual_next
    direction_out[...] = residual_next + new_norm / old_norm * dirs[0]

    for copy in sends + list(row_copies.values()) + part_copies + sums_copies:
        copy.wait_send()


def solution(mesh):
    row_count, col_count = mesh.shape["row"], mesh.shape["col"]

    def body(points, labels, solution, residual, direction, len_low, len_high, *scalars):
        features, width = points.shape
        height = features + 8
        vector = jax.ShapeDtypeStruct((1, width), jnp.float32)
        vmem = pl.BlockSpec(memory_space=pltpu.VMEM)
        smem = pl.BlockSpec(memory_space=pltpu.SMEM)
        dma = pltpu.SemaphoreType.DMA
        outs = pl.pallas_call(
            functools.partial(kernel, row_count, col_count),
            out_shape=(vector,) * 3,
            in_specs=[vmem, smem, vmem, vmem, vmem, vmem, vmem, smem, smem, smem],
            out_specs=(vmem,) * 3,
            scratch_shapes=[
                pltpu.VMEM((row_count, height, width), jnp.float32),
                pltpu.VMEM((col_count, height, width), jnp.float32),
                pltpu.VMEM((2, row_count, width, 4 * features), jnp.bfloat16),
                pltpu.VMEM((2, 4 * features, width), jnp.bfloat16),
                pltpu.VMEM((2, row_count, width, LANES), jnp.float32),
                pltpu.VMEM((2, row_count, width, LANES), jnp.float32),
                pltpu.VMEM((col_count, max(col_count, 8), width), jnp.float32),
                pltpu.VMEM((row_count, 8, LANES), jnp.float32),
                dma((row_count,)),
                dma((row_count,)),
                dma((col_count,)),
                dma((col_count,)),
                dma((col_count,)),
                dma((col_count,)),
                dma((row_count,)),
                dma((row_count,)),
            ],
            compiler_params=pltpu.CompilerParams(
                collective_id=0, has_side_effects=True, vmem_limit_bytes=48 * 1024 * 1024
            ),
        )(
            points,
            labels,
            solution.reshape(1, -1),
            residual.reshape(1, -1),
            direction.reshape(1, -1),
            len_low.reshape(1, -1),
            len_high.reshape(1, -1),
            *scalars,
        )
        return tuple(out.reshape(-1) for out in outs)

    spread = P(("row", "col"))
    return jax.shard_map(
        body,
        mesh=mesh,
        in_specs=(P(None, ("row", "col")), spread, spread, spread, spread) + (P(),) * 5,
        out_specs=(spread,) * 3,
        check_vma=False,
    )
```

time: 172 us -> 33.6 us (0.20)
  blocking collectives: 126 us -> 0 us
  matrix products: 32.1 us -> 0 us
  Pallas kernels: 0 us -> 28.8 us
  between operations: 6.56 us -> 1.36 us
  other arithmetic: 5.15 us -> 0 us
  local copies, waits for them, and re-layouts: 1.28 us -> 3.24 us
    all_gather x7 -> x0, blocking collectives: 77.6 us -> none  [the longest x1 15.7 us: body(): lax.all_gather(own_high, 'col', axis=1, tiled=True)]
    psum x2 -> x0, blocking collectives: 48.4 us -> none  [the longest x1 40 us: body(): lax.psum((jnp.sum(residual * residual), jnp.sum(direction * kernel_image)...]
    dot_general x8 -> x0, matrix products: 32.1 us -> none  [the longest x2 8.99 us: one_block(): jnp.dot(jnp.exp(-0.5 * dist_low), weights_low, precision=lax.Precision.HI...]
    pallas_call x0 -> x1, Pallas kernels: none -> 28.8 us  [body(): pl.pallas_call(functools.partial(kernel, row_count, col_count), out_shape...]
    unnamed x12 -> x21, local copies, waits for them, and re-layouts: 0.03 us -> 3.24 us
where the time goes in v1:
time: 33.6 us; the launch traced here: 33.4 us
  Pallas kernels  28.8 us (86%)
  local copies, waits for them, and re-layouts  3.24 us (10%)
  between operations  1.36 us (4%)
    pallas_call x1, Pallas kernels, body(): pl.pallas_call(functools.partial(kernel, row_count, col_count), out_shape...  28.8 us
    unnamed x21, local copies, waits for them, and re-layouts  3.24 us

profile of v1, /device:TPU:0, one launch (start us, length us, event | category | flops | bytes accessed | tf_op | source)
XLA Modules:
  0.0 33.4 jit_solution(9085003006226457849)
XLA Ops:
  1.3 0.0 copy-start.5
  1.3 0.0 copy-start.6
  1.3 0.0 copy-start.7
  1.3 0.0 copy-start.8
  1.3 0.0 copy-start.2
  1.3 0.0 copy-start.3
  1.3 0.0 copy-start.1
  1.4 0.0 copy-start.4
  1.4 0.6 %copy-done.5 = f32[64]{0:T(128)S(1)} copy-done((f32[64]{0:T(128)S(1)}, f32[64]{0:T(128)}, u32[]{:S(2)}) %copy-start.5) | copy-done | bytes 280
  1.9 0.0 copy-done.6
  2.0 0.0 copy-done.7
  2.0 0.0 copy-done.8
  2.0 0.0 copy-done.2
  2.0 0.0 copy-done.3
  2.0 0.0 copy-done.1
  2.1 0.0 copy-done.4
  2.1 0.0 copy-start
  2.1 0.8 %copy-done = f32[64,256]{1,0:T(8,128)S(1)} copy-done((f32[64,256]{1,0:T(8,128)S(1)}, f32[64,256]{1,0:T(8,128)}, u32[]{:S(2)}) %copy-start) | copy-done | bytes 65560
  2.9 28.8 %shard_map.121 = (f32[1,256]{1,0:T(1,128)S(1)}, f32[1,256]{1,0:T(1,128)S(1)}, f32[1,256]{1,0:T(1,128)S(1)}) custom-call(f32[64,256]{1,0:T(8,128)S(1)} %copy-done, s32[2]{0:T(128)S(1)} %copy-done.4, f32[1,256]{1,0:T(1,128)S(1)} %bitcast.8, f32[1,256]{1,0:T(1,128)S(1)} %bitcast.9, f32[1,256]{1,0:T(1,128)S(1)} %bitcast.10, f32[1,64]{1,0:T(1,128)S(1)} %bitcast.14, ...), custom_call_target="tpu_custom_call" | custom-call | tf_op jit(solution)/shard_map/pallas_call | solution.py:281
  31.7 0.6 %copy.17 = f32[256]{0:T(256)} copy(f32[256]{0:T(256)S(1)} %bitcast.13) | data formatting | bytes 2048
  32.3 0.6 %copy.18 = f32[256]{0:T(256)} copy(f32[256]{0:T(256)S(1)} %bitcast.12) | data formatting | bytes 2048
  32.8 0.6 %copy.19 = f32[256]{0:T(256)} copy(f32[256]{0:T(256)S(1)} %bitcast.11) | data formatting | bytes 2048
Async XLA Ops:
  1.3 0.7 %copy-start.5 = (f32[64]{0:T(128)S(1)}, f32[64]{0:T(128)}, u32[]{:S(2)}) copy-start(f32[64]{0:T(128)} %param.15) | copy-start | bytes 772
  1.3 0.7 %copy-start.6 = (f32[64]{0:T(128)S(1)}, f32[64]{0:T(128)}, u32[]{:S(2)}) copy-start(f32[64]{0:T(128)} %param.16) | copy-start | bytes 772
  1.3 0.7 %copy-start.7 = (f32[2]{0:T(128)S(1)}, f32[2]{0:T(128)}, u32[]{:S(2)}) copy-start(f32[2]{0:T(128)} %variances_ref.1) | copy-start | bytes 28
  1.3 0.7 %copy-start.8 = (f32[2]{0:T(128)S(1)}, f32[2]{0:T(128)}, u32[]{:S(2)}) copy-start(f32[2]{0:T(128)} %nugget_ref.1) | copy-start | bytes 28
  1.3 0.7 %copy-start.2 = (f32[256]{0:T(256)S(1)}, f32[256]{0:T(256)}, u32[]{:S(2)}) copy-start(f32[256]{0:T(256)} %param.13) | copy-start | bytes 3076
  1.3 0.7 %copy-start.3 = (f32[256]{0:T(256)S(1)}, f32[256]{0:T(256)}, u32[]{:S(2)}) copy-start(f32[256]{0:T(256)} %param.14) | copy-start | bytes 3076
  1.3 0.7 %copy-start.1 = (f32[256]{0:T(256)S(1)}, f32[256]{0:T(256)}, u32[]{:S(2)}) copy-start(f32[256]{0:T(256)} %param.12) | copy-start | bytes 3076
  1.4 0.7 %copy-start.4 = (s32[2]{0:T(128)S(1)}, s32[2]{0:T(128)}, u32[]{:S(2)}) copy-start(s32[2]{0:T(128)} %labels_ref.1) | copy-start | bytes 28
  2.1 0.8 %copy-start = (f32[64,256]{1,0:T(8,128)S(1)}, f32[64,256]{1,0:T(8,128)}, u32[]{:S(2)}) copy-start(f32[64,256]{1,0:T(8,128)} %points_ref.1) | copy-start | bytes 196612

commit v2 on v1

--- a/solution.py
+++ b/solution.py
@@ -42,9 +42,19 @@
 def kernel(
     row_count,
     col_count,
-    points_ref,
+    points_hbm,
+    labels_hbm,
+    residual_hbm,
+    direction_hbm,
+    len_low_hbm,
+    len_high_hbm,
+    variances_hbm,
+    nugget_hbm,
+    coupling_hbm,
+    image_out,
+    step_out,
+    ratio_out,
     labels_ref,
-    solution_ref,
     residual_ref,
     direction_ref,
     len_low_ref,
@@ -52,9 +62,7 @@
     variances_ref,
     nugget_ref,
     coupling_ref,
-    solution_out,
-    residual_out,
-    direction_out,
+    load_sem,
     col_buf,
     row_buf,
     lhs,
@@ -73,7 +81,7 @@
     sums_recv,
 ):
     me_row, me_col = lax.axis_index("row"), lax.axis_index("col")
-    features, width = points_ref.shape
+    features, width = points_hbm.shape
     row_peers = [(d, (peer_of(me_row, d, row_count), me_col)) for d in range(1, row_count)]
     col_peers = [(d, (me_row, peer_of(me_col, d, col_count))) for d in range(1, col_count)]
 
@@ -82,17 +90,34 @@
         pl.semaphore_signal(barrier, inc=1, device_id=peer, device_id_type=MESH)
 
     own = col_buf.at[0]
+    loads = [
+        pltpu.make_async_copy(source, target, load_sem.at[at])
+        for at, (source, target) in enumerate(
+            [
+                (points_hbm, own.at[:features, :]),
+                (labels_hbm, labels_ref),
+                (direction_hbm, direction_ref),
+                (residual_hbm, residual_ref),
+                (len_low_hbm, len_low_ref),
+                (len_high_hbm, len_high_ref),
+                (variances_hbm, variances_ref),
+                (nugget_hbm, nugget_ref),
+                (coupling_hbm, coupling_ref),
+            ]
+        )
+    ]
+    for load in loads:
+        load.start()
+    for load in loads:
+        load.wait()
     lane = lax.broadcasted_iota(jnp.int32, (1, width), 1)
+    labels = labels_ref[...].astype(jnp.float32)
     fidelity = jnp.zeros((1, width), jnp.float32)
-    for block in range(labels_ref.shape[0]):
-        fidelity = jnp.where(
-            lane // LANES == block, labels_ref[block].astype(jnp.float32), fidelity
-        )
-    own[:features, :] = points_ref[...]
+    for block in range(labels.shape[1]):
+        fidelity = jnp.where(lane // LANES == block, labels[:, block : block + 1], fidelity)
     own[features:, :] = jnp.concatenate(
         [fidelity, direction_ref[...], residual_ref[...], jnp.zeros((5, width), jnp.float32)], 0
     )
-    row_buf[0] = own[...]
 
     pl.semaphore_wait(barrier, len(row_peers) + len(col_peers))
 
@@ -111,25 +136,32 @@
         sends[-1].start()
     col_copies = dict(zip([d for d, _ in col_peers], sends))
     row_copies = {}
-    for d, peer in row_peers:
+
+    def send_row(source, d, slot):
         copy = pltpu.make_async_remote_copy(
-            src_ref=own,
-            dst_ref=col_buf.at[d],
-            send_sem=row_send.at[d],
-            recv_sem=row_recv.at[d],
-            device_id=peer,
+            src_ref=source,
+            dst_ref=col_buf.at[slot],
+            send_sem=row_send.at[slot],
+            recv_sem=row_recv.at[slot],
+            device_id=(peer_of(me_row, d, row_count), me_col),
             device_id_type=MESH,
         )
         copy.start()
-        row_copies[d] = copy
+        row_copies[slot] = copy
+
+    paired = row_count > 1 and row_count & (row_count - 1) == 0
+    straight = [d for d in range(2, row_count, 2)] + [1] if paired else list(range(1, row_count))
+    for d in straight:
+        send_row(own, d, d)
 
     inverse = [ROOT_LOG2E / len_low_ref[...], ROOT_LOG2E / len_high_ref[...]]
     lane_scale = [jnp.concatenate([value, value], 1) for value in inverse]
     column_scale = [as_column(value) for value in inverse]
-    coupling = coupling_ref[0]
+    coupling = coupling_ref[...]
+    row_blocks = [own] + [row_buf.at[d] for d in range(1, col_count)]
 
     def prepare_rows(d):
-        raw = row_buf[d, :features, :]
+        raw = row_blocks[d][:features, :]
         for which in range(2):
             hi, lo, whole = two_terms(raw * column_scale[which])
             rhs[which] = jnp.concatenate([hi, lo, hi, lo], 0)
@@ -168,19 +200,30 @@
     zeros = jnp.zeros((8, width), jnp.float32)
 
     def finish(d, totals):
-        label = row_buf[d, features : features + 1, :]
+        label = row_blocks[d][features : features + 1, :]
         low = jnp.sum(totals[0], 0, keepdims=True)
         high = jnp.sum(totals[1], 0, keepdims=True)
         part_buf[0, d : d + 1, :] = (
-            variances_ref[0] * (1.0 + (coupling - 1.0) * label) * low
-            + variances_ref[1] * label * high
+            variances_ref[:, 0:1] * (1.0 + (coupling - 1.0) * label) * low
+            + variances_ref[:, 1:2] * label * high
         )
 
     row_bias = list(prepare_rows(0))
     totals = (zeros, zeros)
     prepare_columns(0)
     totals = accumulate(0, row_bias, totals)
-    for d in range(1, row_count):
+    if paired:
+        order = [1] + straight[:-1]
+        for d in order:
+            row_copies[d].wait_recv()
+            if d > 1:
+                send_row(col_buf.at[d], 1, d + 1)
+            prepare_columns(d)
+            totals = accumulate(d, row_bias, totals)
+        rest = list(range(3, row_count, 2))
+    else:
+        rest = list(range(1, row_count))
+    for d in rest:
         row_copies[d].wait_recv()
         prepare_columns(d)
         totals = accumulate(d, row_bias, totals)
@@ -189,7 +232,7 @@
         col_copies[c].wait_recv()
         row_bias = list(prepare_rows(c))
         totals = lax.fori_loop(
-            0, row_count, lambda d, t: accumulate(d, row_bias, t), (zeros, zeros)
+            0, row_count, lambda d, t: accumulate(d, row_bias, t), (zeros, zeros), unroll=True
         )
         finish(c, totals)
 
@@ -206,12 +249,12 @@
         copy.start()
         part_copies.append(copy)
 
-    first, second = nugget_ref[0], nugget_ref[1]
+    first, second = nugget_ref[:, 0:1], nugget_ref[:, 1:2]
     images, labels_of, dirs, resids = [], [], [], []
     for d in range(col_count):
-        labels_of.append(row_buf[d, features : features + 1, :])
-        dirs.append(row_buf[d, features + 1 : features + 2, :])
-        resids.append(row_buf[d, features + 2 : features + 3, :])
+        labels_of.append(row_blocks[d][features : features + 1, :])
+        dirs.append(row_blocks[d][features + 1 : features + 2, :])
+        resids.append(row_blocks[d][features + 2 : features + 3, :])
         images.append(
             part_buf[0, d : d + 1, :] + (first + (second - first) * labels_of[d]) * dirs[d]
         )
@@ -259,10 +302,9 @@
     cross_term, image_norm = sums[2:3], sums[3:4]
     step_size = old_norm / curvature
     new_norm = old_norm - 2.0 * step_size * cross_term + step_size * step_size * image_norm
-    residual_next = resids[0] - step_size * images[0]
-    solution_out[...] = solution_ref[...] + step_size * dirs[0]
-    residual_out[...] = residual_next
-    direction_out[...] = residual_next + new_norm / old_norm * dirs[0]
+    image_out[...] = images[0]
+    step_out[...] = jnp.broadcast_to(step_size, (1, width))
+    ratio_out[...] = jnp.broadcast_to(new_norm / old_norm, (1, width))
 
     for copy in sends + list(row_copies.values()) + part_copies + sums_copies:
         copy.wait_send()
@@ -274,16 +316,20 @@
     def body(points, labels, solution, residual, direction, len_low, len_high, *scalars):
         features, width = points.shape
         height = features + 8
-        vector = jax.ShapeDtypeStruct((1, width), jnp.float32)
         vmem = pl.BlockSpec(memory_space=pltpu.VMEM)
-        smem = pl.BlockSpec(memory_space=pltpu.SMEM)
         dma = pltpu.SemaphoreType.DMA
-        outs = pl.pallas_call(
+        operands = [points] + [
+            value.reshape(1, -1)
+            for value in (labels, residual, direction, len_low, len_high, *scalars)
+        ]
+        image, step_size, ratio = pl.pallas_call(
             functools.partial(kernel, row_count, col_count),
-            out_shape=(vector,) * 3,
-            in_specs=[vmem, smem, vmem, vmem, vmem, vmem, vmem, smem, smem, smem],
+            out_shape=(jax.ShapeDtypeStruct((1, width), jnp.float32),) * 3,
+            in_specs=[pl.BlockSpec(memory_space=pltpu.HBM)] * len(operands),
             out_specs=(vmem,) * 3,
-            scratch_shapes=[
+            scratch_shapes=[pltpu.VMEM(value.shape, value.dtype) for value in operands[1:]]
+            + [
+                dma((len(operands),)),
                 pltpu.VMEM((row_count, height, width), jnp.float32),
                 pltpu.VMEM((col_count, height, width), jnp.float32),
                 pltpu.VMEM((2, row_count, width, 4 * features), jnp.bfloat16),
@@ -302,19 +348,12 @@
                 dma((row_count,)),
             ],
             compiler_params=pltpu.CompilerParams(
-                collective_id=0, has_side_effects=True, vmem_limit_bytes=48 * 1024 * 1024
+                collective_id=0, has_side_effects=True
             ),
-        )(
-            points,
-            labels,
-            solution.reshape(1, -1),
-            residual.reshape(1, -1),
-            direction.reshape(1, -1),
-            len_low.reshape(1, -1),
-            len_high.reshape(1, -1),
-            *scalars,
-        )
-        return tuple(out.reshape(-1) for out in outs)
+        )(*operands)
+        image, step_size, ratio = (value.reshape(-1) for value in (image, step_size, ratio))
+        residual_next = residual - step_size * image
+        return solution + step_size * direction, residual_next, residual_next + ratio * direction
 
     spread = P(("row", "col"))
     return jax.shard_map(

time: 33.6 us -> 27.4 us (0.82)
  Pallas kernels: 28.8 us -> 24.6 us
  local copies, waits for them, and re-layouts: 3.24 us -> 0.69 us
  other arithmetic: 0 us -> 0.57 us
    pallas_call x1, Pallas kernels: 28.8 us -> 24.6 us  [body(): pl.pallas_call(functools.partial(kernel, row_count, col_count), out_shape...]
    unnamed x21 -> x12, local copies, waits for them, and re-layouts: 3.24 us -> 0.69 us
    add x0 -> x1, other arithmetic: none -> 0.57 us  [body(): residual_next + ratio * direction]
where the time goes in v2:
time: 27.4 us; the launch traced here: 27.2 us
  Pallas kernels  24.6 us (90%)
  between operations  1.34 us (5%)
  local copies, waits for them, and re-layouts  0.69 us (3%)
  other arithmetic  0.57 us (2%)
    pallas_call x1, Pallas kernels, body(): pl.pallas_call(functools.partial(kernel, row_count, col_count), out_shape...  24.6 us
    unnamed x12, local copies, waits for them, and re-layouts  0.69 us
    add x1, other arithmetic, body(): residual_next + ratio * direction  0.57 us

profile of v2, /device:TPU:0, one launch (start us, length us, event | category | flops | bytes accessed | tf_op | source)
XLA Modules:
  0.0 27.2 jit_solution(7302326606884275022)
XLA Ops:
  1.3 24.6 %shard_map.121 = (f32[1,256]{1,0:T(1,128)}, f32[1,256]{1,0:T(1,128)}, f32[1,256]{1,0:T(1,128)}) custom-call(f32[64,256]{1,0:T(8,128)} %points_hbm.1, s32[1,2]{1,0:T(1,128)} %bitcast.17, f32[1,256]{1,0:T(1,128)} %bitcast.12, f32[1,256]{1,0:T(1,128)} %bitcast.13, f32[1,64]{1,0:T(1,128)} %bitcast.18, f32[1,64]{1,0:T(1,128)} %bitcast.19, f32[1,2]{1,0:T(1,128)} %bitcast.20, ...), custom_call_target="tpu_custom_call" | custom-call | tf_op jit(solution)/shard_map/pallas_call | solution.py:325
  25.9 0.0 copy-start.5
  25.9 0.0 copy-start.3
  25.9 0.0 copy-start.4
  25.9 0.0 copy-start.1
  25.9 0.0 copy-start.2
  25.9 0.0 copy-start
  25.9 0.6 %copy-done.5 = f32[1,256]{1,0:T(1,128)S(1)} copy-done((f32[1,256]{1,0:T(1,128)S(1)}, f32[1,256]{1,0:T(1,128)}, u32[]{:S(2)}) %copy-start.5) | copy-done | bytes 1048
  26.5 0.0 copy-done.3
  26.5 0.0 copy-done.4
  26.6 0.0 copy-done.1
  26.6 0.0 copy-done.2
  26.6 0.0 copy-done
  26.6 0.6 %multiply_add_fusion = (f32[256]{0:T(256)}, f32[256]{0:T(256)}, f32[256]{0:T(256)}) fusion(f32[256]{0:T(256)S(1)} %bitcast.16, f32[256]{0:T(256)S(1)} %copy-done.1, f32[256]{0:T(256)S(1)} %copy-done, f32[256]{0:T(256)S(1)} %bitcast.15, f32[256]{0:T(256)S(1)} %bitcast.14, f32[256]{0:T(256)S(1)} %copy-done.2), kind=kLoop, calls=%fused_computation | loop fusion | flops 1536 | bytes 9216 | tf_op jit(solution)/shard_map/add | solution.py:356
Async XLA Ops:
  25.9 0.7 %copy-start.5 = (f32[1,256]{1,0:T(1,128)S(1)}, f32[1,256]{1,0:T(1,128)}, u32[]{:S(2)}) copy-start(f32[1,256]{1,0:T(1,128)} %get-tuple-element.8) | copy-start | bytes 3076
  25.9 0.7 %copy-start.3 = (f32[1,256]{1,0:T(1,128)S(1)}, f32[1,256]{1,0:T(1,128)}, u32[]{:S(2)}) copy-start(f32[1,256]{1,0:T(1,128)} %get-tuple-element.7) | copy-start | bytes 3076
  25.9 0.7 %copy-start.4 = (f32[1,256]{1,0:T(1,128)S(1)}, f32[1,256]{1,0:T(1,128)}, u32[]{:S(2)}) copy-start(f32[1,256]{1,0:T(1,128)} %get-tuple-element.6) | copy-start | bytes 3076
  25.9 0.7 %copy-start.1 = (f32[256]{0:T(256)S(1)}, f32[256]{0:T(256)}, u32[]{:S(2)}) copy-start(f32[256]{0:T(256)} %param.14) | copy-start | bytes 3076
  25.9 0.7 %copy-start.2 = (f32[256]{0:T(256)S(1)}, f32[256]{0:T(256)}, u32[]{:S(2)}) copy-start(f32[256]{0:T(256)} %param.12) | copy-start | bytes 3076
  25.9 0.7 %copy-start = (f32[256]{0:T(256)S(1)}, f32[256]{0:T(256)}, u32[]{:S(2)}) copy-start(f32[256]{0:T(256)} %param.13) | copy-start | bytes 3076

commit v3 on v2

--- a/solution.py
+++ b/solution.py
@@ -121,8 +121,9 @@
 
     pl.semaphore_wait(barrier, len(row_peers) + len(col_peers))
 
+    col_order = [0] + [col_count - 1][: col_count - 1] + list(range(1, col_count - 1))
     sends = []
-    for d, peer in col_peers:
+    for d, peer in [col_peers[d - 1] for d in col_order[1:]]:
         sends.append(
             pltpu.make_async_remote_copy(
                 src_ref=own,
@@ -134,7 +135,7 @@
             )
         )
         sends[-1].start()
-    col_copies = dict(zip([d for d, _ in col_peers], sends))
+    col_copies = dict(zip(col_order[1:], sends))
     row_copies = {}
 
     def send_row(source, d, slot):
@@ -198,15 +199,27 @@
         return tuple(result)
 
     zeros = jnp.zeros((8, width), jnp.float32)
+    part_copies = {}
 
     def finish(d, totals):
         label = row_blocks[d][features : features + 1, :]
         low = jnp.sum(totals[0], 0, keepdims=True)
         high = jnp.sum(totals[1], 0, keepdims=True)
-        part_buf[0, d : d + 1, :] = (
+        part_buf[0, d] = (
             variances_ref[:, 0:1] * (1.0 + (coupling - 1.0) * label) * low
             + variances_ref[:, 1:2] * label * high
         )
+        for e, peer in col_peers:
+            copy = pltpu.make_async_remote_copy(
+                src_ref=part_buf.at[0, d],
+                dst_ref=part_buf.at[e, d],
+                send_sem=part_send.at[e, d],
+                recv_sem=part_recv.at[e, d],
+                device_id=peer,
+                device_id_type=MESH,
+            )
+            copy.start()
+            part_copies[e, d] = copy
 
     row_bias = list(prepare_rows(0))
     totals = (zeros, zeros)
@@ -228,26 +241,13 @@
         prepare_columns(d)
         totals = accumulate(d, row_bias, totals)
     finish(0, totals)
-    for c in range(1, col_count):
+    for c in col_order[1:]:
         col_copies[c].wait_recv()
         row_bias = list(prepare_rows(c))
         totals = lax.fori_loop(
             0, row_count, lambda d, t: accumulate(d, row_bias, t), (zeros, zeros), unroll=True
         )
         finish(c, totals)
-
-    part_copies = []
-    for d, peer in col_peers:
-        copy = pltpu.make_async_remote_copy(
-            src_ref=part_buf.at[0],
-            dst_ref=part_buf.at[d],
-            send_sem=part_send.at[d],
-            recv_sem=part_recv.at[d],
-            device_id=peer,
-            device_id_type=MESH,
-        )
-        copy.start()
-        part_copies.append(copy)
 
     first, second = nugget_ref[:, 0:1], nugget_ref[:, 1:2]
     images, labels_of, dirs, resids = [], [], [], []
@@ -256,16 +256,13 @@
         dirs.append(row_blocks[d][features + 1 : features + 2, :])
         resids.append(row_blocks[d][features + 2 : features + 3, :])
         images.append(
-            part_buf[0, d : d + 1, :] + (first + (second - first) * labels_of[d]) * dirs[d]
-        )
-    for d, copy in enumerate(part_copies, 1):
-        copy.wait_recv()
-        for e in range(col_count):
-            if col_count & (col_count - 1):
-                place = (e - d) % col_count
-                images[e] = images[e] + part_buf[d, place : place + 1, :]
-            else:
-                images[e] = images[e] + part_buf[d, (d ^ e) : (d ^ e) + 1, :]
+            part_buf[0, d] + (first + (second - first) * labels_of[d]) * dirs[d]
+        )
+    for place in col_order:
+        for d in range(1, col_count):
+            e = place ^ d if col_count & (col_count - 1) == 0 else (place + d) % col_count
+            part_copies[d, place].wait_recv()
+            images[e] = images[e] + part_buf[d, place]
 
     def line_sum(left, right):
         total = sum(a * b for a, b in zip(left, right))
@@ -277,7 +274,6 @@
             line_sum(dirs, images),
             line_sum(resids, images),
             line_sum(images, images),
-            jnp.zeros((4, LANES), jnp.float32),
         ],
         0,
     )
@@ -306,7 +302,7 @@
     step_out[...] = jnp.broadcast_to(step_size, (1, width))
     ratio_out[...] = jnp.broadcast_to(new_norm / old_norm, (1, width))
 
-    for copy in sends + list(row_copies.values()) + part_copies + sums_copies:
+    for copy in sends + [*row_copies.values(), *part_copies.values()] + sums_copies:
         copy.wait_send()
 
 
@@ -336,14 +332,14 @@
                 pltpu.VMEM((2, 4 * features, width), jnp.bfloat16),
                 pltpu.VMEM((2, row_count, width, LANES), jnp.float32),
                 pltpu.VMEM((2, row_count, width, LANES), jnp.float32),
-                pltpu.VMEM((col_count, max(col_count, 8), width), jnp.float32),
-                pltpu.VMEM((row_count, 8, LANES), jnp.float32),
+                pltpu.VMEM((col_count, col_count, 1, width), jnp.float32),
+                pltpu.VMEM((row_count, 4, LANES), jnp.float32),
                 dma((row_count,)),
                 dma((row_count,)),
                 dma((col_count,)),
                 dma((col_count,)),
-                dma((col_count,)),
-                dma((col_count,)),
+                dma((col_count, col_count)),
+                dma((col_count, col_count)),
                 dma((row_count,)),
                 dma((row_count,)),
             ],

time: 27.4 us -> 27.4 us (level)
  no operation moved by 1% of the time
where the time goes in v3:
time: 27.4 us; the launch traced here: 27.2 us
  Pallas kernels  24.6 us (90%)
  between operations  1.34 us (5%)
  local copies, waits for them, and re-layouts  0.69 us (3%)
  other arithmetic  0.57 us (2%)
    pallas_call x1, Pallas kernels, body(): pl.pallas_call(functools.partial(kernel, row_count, col_count), out_shape...  24.6 us
    unnamed x12, local copies, waits for them, and re-layouts  0.69 us
    add x1, other arithmetic, body(): residual_next + ratio * direction  0.57 us

profile of v3, /device:TPU:0, one launch (start us, length us, event | category | flops | bytes accessed | tf_op | source)
XLA Modules:
  0.0 27.2 jit_solution(5292673863388301713)
XLA Ops:
  1.3 24.6 %shard_map.121 = (f32[1,256]{1,0:T(1,128)}, f32[1,256]{1,0:T(1,128)}, f32[1,256]{1,0:T(1,128)}) custom-call(f32[64,256]{1,0:T(8,128)} %points_hbm.1, s32[1,2]{1,0:T(1,128)} %bitcast.17, f32[1,256]{1,0:T(1,128)} %bitcast.12, f32[1,256]{1,0:T(1,128)} %bitcast.13, f32[1,64]{1,0:T(1,128)} %bitcast.18, f32[1,64]{1,0:T(1,128)} %bitcast.19, f32[1,2]{1,0:T(1,128)} %bitcast.20, ...), custom_call_target="tpu_custom_call" | custom-call | tf_op jit(solution)/shard_map/pallas_call | solution.py:321
  25.9 0.0 copy-start.5
  25.9 0.0 copy-start.3
  25.9 0.0 copy-start.4
  25.9 0.0 copy-start.1
  25.9 0.0 copy-start.2
  25.9 0.0 copy-start
  25.9 0.6 %copy-done.5 = f32[1,256]{1,0:T(1,128)S(1)} copy-done((f32[1,256]{1,0:T(1,128)S(1)}, f32[1,256]{1,0:T(1,128)}, u32[]{:S(2)}) %copy-start.5) | copy-done | bytes 1048
  26.5 0.0 copy-done.3
  26.5 0.0 copy-done.4
  26.6 0.0 copy-done.1
  26.6 0.0 copy-done.2
  26.6 0.0 copy-done
  26.6 0.6 %multiply_add_fusion = (f32[256]{0:T(256)}, f32[256]{0:T(256)}, f32[256]{0:T(256)}) fusion(f32[256]{0:T(256)S(1)} %bitcast.16, f32[256]{0:T(256)S(1)} %copy-done.1, f32[256]{0:T(256)S(1)} %copy-done, f32[256]{0:T(256)S(1)} %bitcast.15, f32[256]{0:T(256)S(1)} %bitcast.14, f32[256]{0:T(256)S(1)} %copy-done.2), kind=kLoop, calls=%fused_computation | loop fusion | flops 1536 | bytes 9216 | tf_op jit(solution)/shard_map/add | solution.py:352
Async XLA Ops:
  25.9 0.7 %copy-start.5 = (f32[1,256]{1,0:T(1,128)S(1)}, f32[1,256]{1,0:T(1,128)}, u32[]{:S(2)}) copy-start(f32[1,256]{1,0:T(1,128)} %get-tuple-element.8) | copy-start | bytes 3076
  25.9 0.7 %copy-start.3 = (f32[1,256]{1,0:T(1,128)S(1)}, f32[1,256]{1,0:T(1,128)}, u32[]{:S(2)}) copy-start(f32[1,256]{1,0:T(1,128)} %get-tuple-element.7) | copy-start | bytes 3076
  25.9 0.7 %copy-start.4 = (f32[1,256]{1,0:T(1,128)S(1)}, f32[1,256]{1,0:T(1,128)}, u32[]{:S(2)}) copy-start(f32[1,256]{1,0:T(1,128)} %get-tuple-element.6) | copy-start | bytes 3076
  25.9 0.7 %copy-start.1 = (f32[256]{0:T(256)S(1)}, f32[256]{0:T(256)}, u32[]{:S(2)}) copy-start(f32[256]{0:T(256)} %param.14) | copy-start | bytes 3076
  25.9 0.7 %copy-start.2 = (f32[256]{0:T(256)S(1)}, f32[256]{0:T(256)}, u32[]{:S(2)}) copy-start(f32[256]{0:T(256)} %param.12) | copy-start | bytes 3076
  25.9 0.7 %copy-start = (f32[256]{0:T(256)S(1)}, f32[256]{0:T(256)}, u32[]{:S(2)}) copy-start(f32[256]{0:T(256)} %param.13) | copy-start | bytes 3076
